TPU v7x, 256 devices: a 8x8x2 block of a 8x8x16 slice. The times are simulated.
256 devices in a mesh: group: 2 (over z), tp: 16 (over x, core), dp: 8 (over y).
Axes of the slice: x: 8, y: 8, z: 2, core: 2. Of those that a mesh axis runs over, the one named last changes fastest.
The devices are a block of a 8x8x16 slice.
Arguments:
- patches: bfloat16 [1024, 128, 1280], P(('group', 'tp', 'dp')), parts along dimension 0, may hold values from -38 to 38, as said below
- patch_counts: int32 [1024], P(('group', 'tp', 'dp')), parts along dimension 0, may hold values from 0 to 128, as said below
- encoder_index: int32 [1024], P(('group', 'tp', 'dp')), parts along dimension 0, may hold values from 0 to 7, as said below
- vit_gain: float32 [1280], replicated, may hold values from 0.1 to 1.9
- vit_up: bfloat16 [1280, 5120], P(None, 'tp'), may hold values from -0.15625 to 0.15625
- vit_down: bfloat16 [5120, 1280], P('tp'), may hold values from -0.078125 to 0.078125
- queries: bfloat16 [64, 32, 128], P(('group', 'dp')), parts along dimension 0, may hold values from -20 to 20
- cache_keys: bfloat16 [64, 4, 8192, 128], P(('group', 'dp'), None, 'tp'), parts along dimension 0, may hold values from -6 to 6
- cache_values: bfloat16 [64, 4, 8192, 128], P(('group', 'dp'), None, 'tp'), parts along dimension 0, may hold values from -6 to 6
- new_keys: bfloat16 [64, 4, 128], P(('group', 'dp')), parts along dimension 0, may hold values from -6 to 6
- new_values: bfloat16 [64, 4, 128], P(('group', 'dp')), parts along dimension 0, may hold values from -6 to 6
- kv_lengths: int32 [64], P(('group', 'dp')), parts along dimension 0, may hold values from 2 to 8192, as said below
- out_weight: bfloat16 [4096, 8192], P(None, 'tp'), may hold values from -0.09375 to 0.09375
Outputs:
- embeddings: bfloat16 [768, 128, 1280], P(('group', 'tp', 'dp')), parts along dimension 0
- decoded: bfloat16 [64, 8192], P(('group', 'dp'), 'tp'), parts along dimension 0
There are 2 independent parts, one for each index of `group`. A program takes and returns all parts, laid end to end along the dimension named above; an argument that names none is the same for every part. Nothing has to cross between parts.
Inputs may be any that keep to these rules, and one draw needn't show every extreme that they name: `patches`: draws of spread scale. `patch_counts`: 0 marks an empty slot. Each device holds between 1 and 4 non-empty slots and some device holds 4; each tp row of 8 devices holds exactly 24 non-empty slots; some slot has 128 patches. `encoder_index`: indices into the dp axis within the slot's own tp row. The non-empty slots of one device name distinct encoders, and every encoder is named by exactly 3 non-empty slots of its tp row. Entries of empty slots carry no meaning. `kv_lengths`: some sequence uses all 8192 positions.
All inputs are finite; a program needn't handle non-finite values.
Results may differ from a plain program's by a relative error of at most 0.015.
Values may be sent and summed in bfloat16 or wider, within the bound.
A program may use at most 192 MiB of HBM per device.

v0:
```python
import jax
import jax.numpy as jnp
from jax import lax
from jax.sharding import PartitionSpec as P

RECV_MAX = 3


def gather_turned(arrays, axis, dims):
    turned = [jnp.moveaxis(a, dim, 0) for a, dim in zip(arrays, dims)]
    widths = [t[0].size for t in turned]
    both = jnp.concatenate([t.reshape(-1, w) for t, w in zip(turned, widths)], axis=1)
    whole = lax.all_gather(both, axis, axis=0, tiled=True)
    blocks = jnp.split(whole, [sum(widths[:k]) for k in range(1, len(widths))], axis=1)
    return tuple(
        (
            jnp.moveaxis(b.reshape(-1, *t.shape[1:]), 0, dim)
            for b, t, dim in zip(blocks, turned, dims)
        )
    )


def from_everyone(array, axis):
    copies = jnp.broadcast_to(array, (lax.axis_size(axis), *array.shape))
    return lax.all_to_all(copies, axis, split_axis=0, concat_axis=0, tiled=True)


def over_copies(array, axis):
    everything = from_everyone(array, axis)
    return jnp.max(everything, axis=0)


def over_pieces(array, axis):
    blocks = lax.all_gather(array, axis).astype(jnp.float32)
    return blocks.sum(axis=0)


def quick_gelu(values):
    return values * jax.nn.sigmoid(1.702 * values)


def vit_block(block_rows, vit_gain, vit_up, vit_down):
    xfloat = block_rows.astype(jnp.float32)
    center = xfloat - jnp.mean(xfloat, axis=-1, keepdims=True)
    spread = jnp.mean(center * center, axis=-1, keepdims=True)
    normed = (center * lax.rsqrt(spread + 1e-06) * vit_gain).astype(jnp.bfloat16)
    up_whole, down_whole = gather_turned((vit_up, vit_down), "tp", (1, 0))
    hidden = quick_gelu(jnp.dot(normed, up_whole, preferred_element_type=jnp.float32)).astype(
        jnp.bfloat16
    )
    branch = jnp.dot(hidden, down_whole, preferred_element_type=jnp.float32)
    return (xfloat + branch).astype(jnp.bfloat16)


def mask_rows(blocks, counts):
    keep = jnp.arange(blocks.shape[1], dtype=jnp.int32)[None, :] < counts[:, None]
    return jnp.where(keep[:, :, None], blocks, jnp.zeros_like(blocks))


def place_images(patches, patch_counts, encoder_index, vit_gain, vit_up, vit_down):
    slot_count, row_count, feature_width = patches.shape
    groups = lax.axis_size("dp")
    live_slots = patch_counts > 0
    targets = (jnp.arange(groups, dtype=jnp.int32)[:, None] == encoder_index[None, :]) & live_slots[
        None, :
    ]
    select = targets.astype(jnp.bfloat16)
    outgoing = jnp.dot(
        select,
        patches.reshape(slot_count, row_count * feature_width),
        preferred_element_type=jnp.float32,
    )
    outgoing = outgoing.astype(jnp.bfloat16).reshape(groups, row_count, feature_width)
    sent_counts = jnp.sum(jnp.where(targets, patch_counts[None, :], 0), axis=1).astype(jnp.bfloat16)
    arrived, arrived_counts = (
        lax.all_to_all(outgoing, "dp", split_axis=0, concat_axis=0, tiled=True),
        lax.all_to_all(sent_counts, "dp", split_axis=0, concat_axis=0, tiled=True),
    )
    present = arrived_counts > 0
    ranking = jnp.cumsum(present.astype(jnp.int32)) - 1
    pick_mask = (jnp.arange(RECV_MAX, dtype=jnp.int32)[:, None] == ranking[None, :]) & present[
        None, :
    ]
    picker = pick_mask.astype(jnp.bfloat16)
    gathered = jnp.dot(
        picker,
        arrived.reshape(groups, row_count * feature_width),
        preferred_element_type=jnp.float32,
    )
    gathered = gathered.astype(jnp.bfloat16).reshape(RECV_MAX, row_count, feature_width)
    kept_counts = jnp.sum(
        jnp.where(pick_mask, arrived_counts.astype(jnp.float32)[None, :], 0.0), axis=1
    ).astype(jnp.int32)
    encoded = vit_block(
        gathered.reshape(RECV_MAX * row_count, feature_width), vit_gain, vit_up, vit_down
    )
    gathered = mask_rows(encoded.reshape(RECV_MAX, row_count, feature_width), kept_counts)
    return gathered


def decode_step(queries, cache_keys, cache_values, new_keys, new_values, kv_lengths, out_weight):
    seq_count, kv_heads, span, head_dim = cache_keys.shape
    per_group = queries.shape[1] // kv_heads
    scale = head_dim ** (-0.5)
    grouped = queries.reshape(seq_count, kv_heads, per_group, head_dim)
    positions = lax.axis_index("tp") * span + jnp.arange(span, dtype=jnp.int32)
    valid = positions[None, :] < kv_lengths[:, None]
    scores = (
        jnp.einsum("skgd,skpd->skgp", grouped, cache_keys, preferred_element_type=jnp.float32)
        * scale
    )
    scores = jnp.where(valid[:, None, None, :], scores, -1e30)
    own = jnp.einsum("skgd,skd->skg", grouped, new_keys, preferred_element_type=jnp.float32) * scale
    local_top = jnp.maximum(jnp.max(scores, axis=-1), own)
    top = over_copies(local_top, "tp")
    weights = jnp.exp(scores - top[..., None])
    local_total = jnp.sum(weights, axis=-1)
    local_mix = jnp.einsum(
        "skgp,skpd->skgd",
        weights.astype(jnp.bfloat16),
        cache_values,
        preferred_element_type=jnp.float32,
    )
    total, mixed = (
        over_pieces(local_total.astype(jnp.bfloat16), "tp").astype(jnp.float32),
        over_pieces(local_mix.astype(jnp.bfloat16), "tp").astype(jnp.float32),
    )
    own_weight = jnp.exp(own - top)
    total = total + own_weight
    own_rounded = lax.optimization_barrier(own_weight.astype(jnp.bfloat16)).astype(jnp.float32)
    mixed = mixed + own_rounded[..., None] * new_values.astype(jnp.float32)[:, :, None, :]
    attended = (mixed / total[..., None]).astype(jnp.bfloat16).reshape(seq_count, -1)
    return jnp.dot(attended, out_weight, preferred_element_type=jnp.float32).astype(jnp.bfloat16)


def local(
    patches,
    patch_counts,
    encoder_index,
    vit_gain,
    vit_up,
    vit_down,
    queries,
    cache_keys,
    cache_values,
    new_keys,
    new_values,
    kv_lengths,
    out_weight,
):
    decoded = decode_step(
        queries, cache_keys, cache_values, new_keys, new_values, kv_lengths, out_weight
    )
    embeddings = place_images(patches, patch_counts, encoder_index, vit_gain, vit_up, vit_down)
    return (embeddings, decoded)


def solution(mesh):
    return jax.shard_map(
        local,
        mesh=mesh,
        in_specs=(
            P(("group", "tp", "dp"), None, None),
            P(("group", "tp", "dp")),
            P(("group", "tp", "dp")),
            P(),
            P(None, "tp"),
            P("tp", None),
            P(("group", "dp"), None, None),
            P(("group", "dp"), None, "tp", None),
            P(("group", "dp"), None, "tp", None),
            P(("group", "dp"), None, None),
            P(("group", "dp"), None, None),
            P(("group", "dp")),
            P(None, "tp"),
        ),
        out_specs=(P(("group", "tp", "dp"), None, None), P(("group", "dp"), "tp")),
        check_vma=False,
    )
```

profile of v0, /device:TPU:513, one launch (start us, length us, event | category | flops | bytes accessed | tf_op | source)
XLA Modules:
  0.0 202.3 jit_solution(7990581057906296930)
XLA Ops:
  7.3 2.8 %pad_maximum_fusion = bf16[320,2560]{1,0:T(8,128)(2,1)} fusion(bf16[320,1280]{1,0:T(8,128)(2,1)} %param.18, bf16[320,1280]{1,0:T(8,128)(2,1)} %bitcast.43), kind=kLoop, calls=%fused_computation.14 | loop fusion | flops 3276800 | bytes 3276800 | tf_op jit(solution)/shard_map/concatenate | solution.py:12
  11.0 13.7 %all-to-all-start = ((bf16[8,1,1]{2,1,0:T(2,128)(2,1)}), bf16[8,1,1]{2,1,0:T(2,128)(2,1)S(1)}, u32[]{:S(2)}, u32[]{:S(2)}) async-start(bf16[8,1,1]{2,1,0:T(2,128)(2,1)} %copy.21), calls=%async_computation | async-start | bytes 8192 | tf_op jit(solution)/shard_map/all_to_all | solution.py:77
  24.7 2.3 %copy.27 = bf16[1,4,128,1280]{3,1,2,0:T(4,128)(2,1)S(1)} copy(bf16[1,4,128,1280]{3,2,1,0:T(8,128)(2,1)} %bitcast.41) | data formatting | bytes 2621440
  27.3 1.4 fusion.52
  28.7 0.8 reshape.189
  29.4 1.7 all-to-all-done
  31.2 14.4 %all-to-all-start.2 = ((f32[16,1,128]{2,1,0:T(1,128)}), f32[16,1,128]{2,1,0:T(1,128)S(1)}, u32[]{:S(2)}, u32[]{:S(2)}) async-start(f32[16,1,128]{2,1,0:T(1,128)} %reshape.189), calls=%async_computation.2 | async-start | bytes 16384 | tf_op jit(solution)/shard_map/all_to_all | solution.py:25
  45.6 2.0 %convolution_convert_fusion = bf16[8,163840]{1,0:T(8,128)(2,1)S(1)} fusion(bf16[4,163840]{1,0:T(4,128)(2,1)S(1)} %bitcast.39, s32[4]{0:T(128)S(1)} %copy-done.4, pred[4]{0:T(512)(128)(4,1)} %copy-done.5), kind=kOutput, calls=%fused_computation | convolution fusion | flops 11796544 | bytes 3932180 | tf_op jit(solution)/shard_map/dot_general | solution.py:68
  47.6 2.0 copy.22
  49.6 3.4 %all-to-all-done.2 = f32[16,1,128]{2,1,0:T(1,128)S(1)} async-done(((f32[16,1,128]{2,1,0:T(1,128)}), f32[16,1,128]{2,1,0:T(1,128)S(1)}, u32[]{:S(2)}, u32[]{:S(2)}) %all-to-all-start.2) | async-done | bytes 8224 | tf_op jit(solution)/shard_map/all_to_all | solution.py:25
  53.0 4.6 %all-to-all-start.1 = ((bf16[8,128,1280]{2,1,0:T(8,128)(2,1)}), bf16[8,128,1280]{2,1,0:T(8,128)(2,1)}, u32[]{:S(2)}, u32[]{:S(2)}) async-start(bf16[8,128,1280]{2,1,0:T(8,128)(2,1)} %copy.22), calls=%async_computation.1 | async-start | bytes 5242880 | tf_op jit(solution)/shard_map/all_to_all | solution.py:76
  60.3 16.2 %all-gather.1 = bf16[64,4,8]{2,1,0:T(4,128)(2,1)S(1)} all-gather(bf16[4,4,8]{2,1,0:T(4,128)(2,1)S(1)} %fusion.28), channel_id=3, replica_groups=mesh['group'=2,'tp'=16,'dp'=8] {'tp'}, dimensions={0}, use_global_device_ids=true | all-gather | bytes 4352 | tf_op jit(solution)/shard_map/all_gather | solution.py:34
  76.5 2.1 %convolution_convert_fusion.2 = bf16[4,4,8,128]{3,2,1,0:T(8,128)(2,1)S(1)} fusion(bf16[4,4,512,128]{3,2,1,0:T(8,128)(2,1)} %param.21, f32[4,4,8,512]{3,2,1,0:T(8,128)S(1)} %copy-done.1, f32[4,4,8]{2,1,0:T(4,128)S(1)} %reduce_max.19), kind=kOutput, calls=%fused_computation.17 | convolution fusion | flops 16924672 | bytes 2392576 | tf_op jit(solution)/shard_map/skgp,skpd->skgd/dot_general | solution.py:118
  78.6 20.6 %all-gather = bf16[64,4,8,128]{3,2,1,0:T(8,128)(2,1)S(1)} all-gather(bf16[4,4,8,128]{3,2,1,0:T(8,128)(2,1)S(1)} %convolution_convert_fusion.2), channel_id=2, replica_groups=mesh['group'=2,'tp'=16,'dp'=8] {'tp'}, dimensions={0}, use_global_device_ids=true | all-gather | bytes 557056 | tf_op jit(solution)/shard_map/all_gather | solution.py:34
  99.4 3.4 %convolution_convert_fusion.3 = bf16[4,512]{1,0:T(4,128)(2,1)} fusion(bf16[4096,512]{1,0:T(8,128)(2,1)} %param.25, bf16[1,4,32,128]{3,2,1,0:T(8,128)(2,1)S(1)} %fusion.37), kind=kOutput, calls=%fused_computation.18 | convolution fusion | flops 16779264 | bytes 4231168 | tf_op jit(solution)/shard_map/dot_general | solution.py:133
  102.9 17.7 %all-to-all-done.1 = bf16[8,128,1280]{2,1,0:T(8,128)(2,1)} async-done(((bf16[8,128,1280]{2,1,0:T(8,128)(2,1)}), bf16[8,128,1280]{2,1,0:T(8,128)(2,1)}, u32[]{:S(2)}, u32[]{:S(2)}) %all-to-all-start.1) | async-done | bytes 2621472 | tf_op jit(solution)/shard_map/all_to_all | solution.py:76
  120.6 3.2 %copy.28 = bf16[1,8,128,1280]{3,1,2,0:T(8,128)(2,1)S(1)} copy(bf16[1,8,128,1280]{3,2,1,0:T(8,128)(2,1)} %bitcast.16) | data formatting | bytes 5242880
  123.8 2.3 %fusion = f32[3,163840]{1,0:T(4,128)} fusion(bf16[8,163840]{1,0:T(8,128)(2,1)S(1)} %bitcast.37, s32[8]{0:T(128)S(1)} %add_bitcast_fusion, pred[8]{0:T(512)(128)(4,1)S(1)} %compare_reduce_fusion), kind=kOutput, calls=%fused_computation.2 | convolution fusion | flops 8847408 | bytes 4587560 | tf_op jit(solution)/shard_map/dot_general | solution.py:85
  126.1 4.6 %reshape.179 = f32[384,1280]{1,0:T(8,128)} reshape(f32[3,163840]{1,0:T(4,128)} %fusion) | data formatting | bytes 3932160 | tf_op jit(solution)/shard_map/convert_element_type | solution.py:43
  130.6 1.7 reduce_sum.65
  132.4 1.9 multiply_reduce_fusion
  134.3 39.2 %all-gather.4.cloned.1.call-done = bf16[5120,2560]{1,0:T(8,128)(2,1)} async-done(((bf16[320,2560]{1,0:T(8,128)(2,1)}), bf16[5120,2560]{1,0:T(8,128)(2,1)}) %all-gather.4.cloned.1.call-update) | async-done | bytes 26214416 | tf_op jit(solution)/shard_map/all_gather | solution.py:13
  173.5 20.8 %fusion.16 = bf16[384,1280]{1,0:T(8,128)(2,1)S(1)} fusion(f32[384,1280]{1,0:T(8,128)} %reshape.179, bf16[5120,2560]{1,0:T(8,128)(2,1)} %all-gather.4.cloned.1.call-done, f32[1280]{0:T(1024)S(1)} %copy-done.8, f32[384]{0:T(512)S(1)} %add_rsqrt_fusion, f32[384]{0:T(512)S(1)} %broadcast_multiply_fusion), kind=kOutput, calls=%fused_computation.11 | convolution fusion | flops 10081075200 | bytes 31137792 | tf_op jit(solution)/shard_map/dot_general | solution.py:51
  194.3 1.1 broadcast_select_fusion
  (52 shorter events, 4.1 us)
Async XLA Ops:
  7.2 20.1 %copy-start = (bf16[4,4,512,128]{3,2,1,0:T(8,128)(2,1)S(1)}, bf16[4,4,512,128]{3,2,1,0:T(8,128)(2,1)}, u32[]{:S(2)}) copy-start(bf16[4,4,512,128]{3,2,1,0:T(8,128)(2,1)} %param.20) | copy-start | bytes 6291460
  7.2 3.0 %copy-start.7 = (s32[4]{0:T(128)S(1)}, s32[4]{0:T(128)}, u32[]{:S(2)}) copy-start(s32[4]{0:T(128)} %param.14) | copy-start | bytes 52
  7.2 3.0 %copy-start.4 = (s32[4]{0:T(128)S(1)}, s32[4]{0:T(128)}, u32[]{:S(2)}) copy-start(s32[4]{0:T(128)} %param.15) | copy-start | bytes 52
  7.2 166.3 %all-gather.4.cloned.1.call-start = ((), (), s32[]{:S(2)}) async-start(), calls=%async_computation.3 | async-start | bytes 27852800 | tf_op jit(solution)/shard_map/all_gather | solution.py:13
  10.1 17.0 %copy-start.6 = (s32[4]{0:T(128)S(1)}, s32[4]{0:T(128)}, u32[]{:S(2)}) copy-start(s32[4]{0:T(128)} %param.24) | copy-start | bytes 52
  10.1 17.0 %copy-start.2 = (bf16[4,32,128]{2,1,0:T(8,128)(2,1)S(1)}, bf16[4,32,128]{2,1,0:T(8,128)(2,1)}, u32[]{:S(2)}) copy-start(bf16[4,32,128]{2,1,0:T(8,128)(2,1)} %param.19) | copy-start | bytes 98308
  10.1 17.0 %copy-start.9 = (bf16[4,4,128]{2,1,0:T(4,128)(2,1)S(1)}, bf16[4,4,128]{2,1,0:T(4,128)(2,1)}, u32[]{:S(2)}) copy-start(bf16[4,4,128]{2,1,0:T(4,128)(2,1)} %param.22) | copy-start | bytes 12292
  10.2 16.8 %copy-start.5 = (pred[4]{0:T(512)(128)(4,1)}, pred[4]{0:T(512)(128)(4,1)S(1)}, u32[]{:S(2)}) copy-start(pred[4]{0:T(512)(128)(4,1)S(1)} %broadcast_compare_fusion.1) | copy-start | bytes 16
  11.0 20.2 %all-to-all-start = ((bf16[8,1,1]{2,1,0:T(2,128)(2,1)}), bf16[8,1,1]{2,1,0:T(2,128)(2,1)S(1)}, u32[]{:S(2)}, u32[]{:S(2)}) async-start(bf16[8,1,1]{2,1,0:T(2,128)(2,1)} %copy.21), calls=%async_computation | async-start | bytes 8192 | tf_op jit(solution)/shard_map/all_to_all | solution.py:77
  31.2 21.8 %all-to-all-start.2 = ((f32[16,1,128]{2,1,0:T(1,128)}), f32[16,1,128]{2,1,0:T(1,128)S(1)}, u32[]{:S(2)}, u32[]{:S(2)}) async-start(f32[16,1,128]{2,1,0:T(1,128)} %reshape.189), calls=%async_computation.2 | async-start | bytes 16384 | tf_op jit(solution)/shard_map/all_to_all | solution.py:25
  49.6 8.0 %copy-start.3 = (bf16[4,4,128]{2,1,0:T(4,128)(2,1)S(1)}, bf16[4,4,128]{2,1,0:T(4,128)(2,1)}, u32[]{:S(2)}) copy-start(bf16[4,4,128]{2,1,0:T(4,128)(2,1)} %param.23) | copy-start | bytes 12292
  49.6 10.5 %copy-start.1 = (f32[4,4,8,512]{3,2,1,0:T(8,128)S(1)}, f32[4,4,8,512]{3,2,1,0:T(8,128)}, u32[]{:S(2)}) copy-start(f32[4,4,8,512]{3,2,1,0:T(8,128)} %get-tuple-element.5) | copy-start | bytes 786436
  53.0 67.6 %all-to-all-start.1 = ((bf16[8,128,1280]{2,1,0:T(8,128)(2,1)}), bf16[8,128,1280]{2,1,0:T(8,128)(2,1)}, u32[]{:S(2)}, u32[]{:S(2)}) async-start(bf16[8,128,1280]{2,1,0:T(8,128)(2,1)} %copy.22), calls=%async_computation.1 | async-start | bytes 5242880 | tf_op jit(solution)/shard_map/all_to_all | solution.py:76
  130.6 42.9 %copy-start.8 = (f32[1280]{0:T(1024)S(1)}, f32[1280]{0:T(1024)}, u32[]{:S(2)}) copy-start(f32[1280]{0:T(1024)} %param.16) | copy-start | bytes 15364
Sparse Core Ops, SparseCore 0:
  10.3 163.1 all-gather.3
where the time goes:
time: 203 us; the launch traced here: 202 us
  waiting for transfers between devices  62 us (31%)
  blocking collectives  36.8 us (18%)
  starting transfers between devices  32.8 us (16%)
  matrix products  32.2 us (16%)
  local copies, waits for them, and re-layouts  14.3 us (7%)
  between operations  14.3 us (7%)
  other arithmetic  9.94 us (5%)
    all_gather x1, waiting for transfers between devices, gather_turned(): whole = lax.all_gather(both, axis, axis=0, tiled=True)  39.2 us
    all_gather x2, blocking collectives, over_pieces(): blocks = lax.all_gather(array, axis).astype(jnp.float32)  36.8 us
    dot_general x1, matrix products, vit_block(): branch = jnp.dot(hidden, down_whole, preferred_element_type=jnp.float32)  20.8 us
    all_to_all x1, waiting for transfers between devices, place_images(): lax.all_to_all(outgoing, 'dp', split_axis=0, concat_axis=0, tiled=True)  17.7 us
    all_to_all x1, starting transfers between devices, from_everyone(): return lax.all_to_all(copies, axis, split_axis=0, concat_axis=0, tiled=True)  14.4 us
    all_to_all x1, starting transfers between devices, place_images(): lax.all_to_all(sent_counts, 'dp', split_axis=0, concat_axis=0, tiled=True)  13.7 us
    unnamed x24, local copies, waits for them, and re-layouts  6.52 us
    all_to_all x1, starting transfers between devices, place_images(): lax.all_to_all(outgoing, 'dp', split_axis=0, concat_axis=0, tiled=True)  4.58 us
  transfers between devices with their start and end apart: 4, of which 4 were waited for; matrix products, arithmetic and copies ran while one was open for 16% of the time, Pallas kernels for 0%

commit v1 on v0

v1 whole, which is shorter than its diff:
```python
import functools

import jax
import jax.numpy as jnp
from jax import lax
from jax.experimental import pallas as pl
from jax.experimental.pallas import tpu as pltpu
from jax.sharding import PartitionSpec as P

MESH = pl.DeviceIdType.MESH
RECV_MAX = 3
CORES = 2
F32 = jnp.float32
BF16 = jnp.bfloat16


def rcopy(src, dst, send, recv, **where):
    return pltpu.make_async_remote_copy(
        src_ref=src,
        dst_ref=dst,
        send_sem=send,
        recv_sem=recv,
        device_id=where,
        device_id_type=MESH,
    )


def drain(ref, sem):
    pltpu.make_async_copy(ref, ref, sem).wait()


def kernel(
    sizes,
    counts,
    enc,
    lens,
    patches,
    gain,
    up,
    down,
    q,
    keys,
    values,
    nk,
    nv,
    ow,
    emb,
    dec,
    w,
    upv,
    pv,
    outgoing,
    arrived,
    kv,
    vv,
    owv,
    meta_out,
    meta_in,
    meta_s,
    rs_src,
    rs_dst,
    ag_dst,
    own_buf,
    nv_buf,
    normed,
    acc,
    local_sem,
    x_recv,
    z_recv,
    d_recv,
    x_send,
    z_send,
    d_send,
    da_send,
    dz_send,
    a_sem,
    m_sem,
    rs_sem,
    ag_sem,
):
    n_tp, n_dp, paired = sizes
    ring = n_tp // CORES
    hops = ring - 1
    half = w.shape[3]
    zrows = (half * 3 // 10) // 16 * 16 if paired else 0
    xrows = half - zrows
    t = lax.axis_index("tp")
    y = lax.axis_index("dp")
    g = lax.axis_index("group")
    par = lax.rem(g, 2)
    right = lax.rem(t + CORES, n_tp)
    left = lax.rem(t + n_tp - CORES, n_tp)
    sib = t + 1 - 2 * lax.rem(t, 2)
    peer = g + 1 - 2 * par
    xstart = pl.multiple_of(par * zrows, 16)
    zstart = pl.multiple_of(par * xrows, 16)
    zother = pl.multiple_of((1 - par) * xrows, 16)
    slots = patches.shape[0]

    barrier = pltpu.get_barrier_semaphore()
    for d in range(1, n_tp):
        pl.semaphore_signal(
            barrier, inc=1, device_id={"tp": lax.rem(t + d, n_tp)}, device_id_type=MESH
        )
    for d in range(1, n_dp):
        pl.semaphore_signal(
            barrier, inc=1, device_id={"dp": lax.rem(y + d, n_dp)}, device_id_type=MESH
        )
    if paired:
        pl.semaphore_signal(barrier, inc=1, device_id={"group": peer}, device_id_type=MESH)

    loads = [
        pltpu.make_async_copy(up, upv, local_sem.at[0]),
        pltpu.make_async_copy(down.at[pl.ds(0, half)], w.at[1, 0, 0], local_sem.at[1]),
        pltpu.make_async_copy(down.at[pl.ds(half, half)], w.at[1, 0, 1], local_sem.at[2]),
        pltpu.make_async_copy(patches, pv, local_sem.at[3]),
        pltpu.make_async_copy(keys, kv, local_sem.at[4]),
        pltpu.make_async_copy(values, vv, local_sem.at[5]),
        pltpu.make_async_copy(ow, owv, local_sem.at[6]),
    ]
    for load in loads:
        load.start()

    row = lax.broadcasted_iota(jnp.int32, (8, 128), 0)
    lane = lax.broadcasted_iota(jnp.int32, (8, 128), 1)
    meta = jnp.zeros((8, 128), jnp.int32)
    for s in range(slots):
        meta = jnp.where((row == 0) & (lane == s), counts[s], meta)
        meta = jnp.where((row == 1) & (lane == s), enc[s], meta)
    meta_out[...] = meta
    meta_in[y] = meta

    loads[0].wait()
    w[0, 0, 0:2] = jnp.transpose(upv[...].astype(F32)).astype(BF16).reshape(2, half, upv.shape[0])

    pl.semaphore_wait(barrier, n_tp - 1 + n_dp - 1 + (1 if paired else 0))

    def x_copy(lane_, d, r):
        rows = pl.ds(xstart, xrows)
        return rcopy(
            w.at[lane_, r, d, rows],
            w.at[lane_, r + 1, d, rows],
            x_send,
            x_recv.at[lane_, d, r],
            tp=right if d == 0 else left,
        )

    def z_copy(lane_, d, r):
        rows = pl.ds(zstart, zrows)
        return rcopy(
            w.at[lane_, r, d, rows],
            w.at[lane_, r, d, rows],
            z_send,
            z_recv.at[lane_, d, r],
            group=peer,
        )

    def d_copy(lane_, d, r, part):
        rows, send = {
            0: (pl.ds(xstart, xrows), d_send),
            1: (pl.ds(zother, zrows), dz_send),
            2: (pl.ds(0, half), da_send),
        }[part]
        return rcopy(
            w.at[lane_, r, d, rows],
            w.at[lane_, r, 2 + d, rows],
            send,
            d_recv.at[lane_, d, r, min(part, 1) if part < 2 else 0],
            tp=sib,
        )

    loads[1].wait()
    loads[2].wait()
    for lane_ in (1, 0):
        for d in (0, 1):
            x_copy(lane_, d, 0).start()

    loads[3].wait()

    def stage(e, carry):
        slot = jnp.int32(0)
        for s in range(slots):
            slot = slot + jnp.where((counts[s] > 0) & (enc[s] == e), s, 0)
        outgoing[e] = pv[slot]
        return carry

    lax.fori_loop(0, n_dp, stage, 0)
    for d in range(1, n_dp):
        to = lax.rem(y + d, n_dp)
        rcopy(meta_out, meta_in.at[y], m_sem.at[0], m_sem.at[1], dp=to).start()
    far_first = sorted(range(1, n_dp), key=lambda d: -min(d, n_dp - d))
    for d in far_first:
        to = lax.rem(y + d, n_dp)
        rcopy(outgoing.at[to], arrived.at[y], a_sem.at[0], a_sem.at[1], dp=to).start()
    arrived[y] = outgoing[y]
    for lane_ in (1, 0):
        for d in (0, 1):
            d_copy(lane_, d, 0, 2).start()

    seqs, kvh, span, hd = kv.shape
    per = q.shape[1] // kvh
    scale = hd**-0.5
    own_heads = (kvh * per) // n_tp

    def attend_local():
        loads[4].wait()
        loads[5].wait()
        wide = lax.broadcasted_iota(jnp.int32, (per, 128), 1)
        for s in range(seqs):
            pos = t * span + lax.broadcasted_iota(jnp.int32, (per, span), 1)
            valid = pos < lens[s]
            for h in range(kvh):
                query = q[s, h * per : (h + 1) * per, :]
                scores = (
                    lax.dot_general(
                        query, kv[s, h], (((1,), (1,)), ((), ())), preferred_element_type=F32
                    )
                    * scale
                )
                scores = jnp.where(valid, scores, -1e30)
                own = (
                    jnp.sum(
                        query.astype(F32) * nk[s, h : h + 1, :].astype(F32), axis=1, keepdims=True
                    )
                    * scale
                )
                top = jnp.maximum(jnp.max(scores, axis=1, keepdims=True), own)
                weights = jnp.exp(scores - top)
                total = jnp.sum(weights, axis=1, keepdims=True)
                mix = jnp.dot(weights.astype(BF16), vv[s, h], preferred_element_type=F32)
                stats = jnp.where(wide < 64, top, total)
                ownw = jnp.broadcast_to(own, (per, 128))
                fresh = nv[s, h : h + 1, :].astype(F32)
                for i in range(per):
                    head = h * per + i
                    p, j = head // own_heads, head % own_heads
                    at = seqs * j + s
                    rs_src[p, at : at + 1, :] = mix[i : i + 1, :]
                    rs_src[p, 8 + at : 9 + at, :] = stats[i : i + 1, :]
                    own_buf[p, at : at + 1, :] = ownw[i : i + 1, :]
                    nv_buf[p, at : at + 1, :] = fresh
        rs_dst[t] = rs_src[t]
        for d in range(1, n_tp):
            to = lax.rem(t + d, n_tp)
            rcopy(rs_src.at[to], rs_dst.at[t], rs_sem.at[0], rs_sem.at[1], tp=to).start()

    def attend_merge():
        some = pl.ds(0, n_tp - 1)
        drain(rs_dst.at[some], rs_sem.at[1])
        own = own_buf[t][:, 0:1]
        tops = [rs_dst[p, 8:16, 0:1] for p in range(n_tp)]
        top = own
        for m in tops:
            top = jnp.maximum(top, m)
        own_weight = jnp.exp(own - top)
        total = own_weight
        mixed = own_weight.astype(BF16).astype(F32) * nv_buf[t]
        for p in range(n_tp):
            factor = jnp.exp(tops[p] - top)
            total = total + rs_dst[p, 8:16, 64:65] * factor
            mixed = mixed + rs_dst[p, 0:8, :] * factor
        ag_dst[t] = (mixed / total).astype(BF16).astype(F32)
        for d in range(1, n_tp):
            to = lax.rem(t + d, n_tp)
            rcopy(ag_dst.at[t], ag_dst.at[t], ag_sem.at[0], ag_sem.at[1], tp=to).start()

    def project():
        loads[6].wait()
        drain(ag_dst.at[pl.ds(0, n_tp - 1)], ag_sem.at[1])
        wide = own_heads * hd
        total = jnp.zeros((8, owv.shape[1]), F32)
        which = lax.broadcasted_iota(jnp.int32, (8, hd), 0) // seqs
        for p in range(n_tp):
            block = ag_dst[p]
            lhs = jnp.concatenate(
                [jnp.where(which == j, block, 0.0) for j in range(own_heads)], axis=1
            ).astype(BF16)
            total = total + jnp.dot(
                lhs, owv[p * wide : (p + 1) * wide, :], preferred_element_type=F32
            )
        out = total[0:seqs]
        for j in range(1, own_heads):
            out = out + total[j * seqs : (j + 1) * seqs]
        dec[...] = out.astype(BF16)

    kept = []

    def images():
        drain(meta_in.at[pl.ds(0, n_dp - 1)], m_sem.at[1])
        small = pltpu.make_async_copy(meta_in, meta_s, local_sem.at[7])
        small.start()
        small.wait()
        drain(arrived.at[pl.ds(0, n_dp - 1)], a_sem.at[1])
        found = jnp.int32(0)
        pick = [jnp.int32(0)] * RECV_MAX
        keep = [jnp.int32(0)] * RECV_MAX
        for src in range(n_dp):
            count = jnp.int32(0)
            for s in range(slots):
                c = meta_s[src, 0, s]
                count = count + jnp.where((c > 0) & (meta_s[src, 1, s] == y), c, 0)
            for k in range(RECV_MAX):
                hit = (count > 0) & (found == k)
                pick[k] = jnp.where(hit, src, pick[k])
                keep[k] = jnp.where(hit, count, keep[k])
            found = found + jnp.where(count > 0, 1, 0)
        kept.extend(keep)
        rows = arrived.shape[1]
        for k in range(RECV_MAX):
            x = arrived[pick[k]].astype(F32)
            acc[k * rows : (k + 1) * rows, :] = x
            center = x - jnp.mean(x, axis=1, keepdims=True)
            spread = jnp.mean(center * center, axis=1, keepdims=True)
            n = (center * lax.rsqrt(spread + 1e-06) * gain[...]).astype(BF16)
            normed[k * rows : (k + 1) * rows, :] = n

    def vit(r):
        width = w.shape[4]
        a = w[0, r].reshape(4 * half, width)
        pre = lax.dot_general(
            normed[...], a, (((1,), (1,)), ((), ())), preferred_element_type=F32
        )
        hidden = (pre * jax.nn.sigmoid(1.702 * pre)).astype(BF16)
        b = w[1, r].reshape(4 * half, width)
        acc[...] += jnp.dot(hidden, b, preferred_element_type=F32)

    def vit_range(lo, hi):
        def body(r, carry):
            vit(r)
            return carry

        lax.fori_loop(lo, hi, body, 0)

    def finish(r):
        if paired:
            for lane_ in (1, 0):
                for d in (0, 1):
                    drain(w.at[lane_, r, d, pl.ds(zother, zrows)], z_recv.at[lane_, d, r])
                    d_copy(lane_, d, r, 1).start()

    def ready(r):
        for lane_ in (1, 0):
            for d in (0, 1):
                if r == 0:
                    drain(w.at[lane_, r, 2 + d], d_recv.at[lane_, d, r, 0])
                else:
                    drain(w.at[lane_, r, 2 + d, pl.ds(xstart, xrows)], d_recv.at[lane_, d, r, 0])
                    if paired:
                        drain(
                            w.at[lane_, r, 2 + d, pl.ds(zother, zrows)], d_recv.at[lane_, d, r, 1]
                        )

    work = {1: attend_local, 2: attend_merge, 3: project}
    first_vit = max(hops - 2, 4)
    for r in range(1, hops + 1):
        for lane_ in (1, 0):
            for d in (0, 1):
                rows = pl.ds(xstart, xrows)
                drain(w.at[lane_, r, d, rows], x_recv.at[lane_, d, r - 1])
                if r < hops:
                    x_copy(lane_, d, r).start()
                if paired:
                    z_copy(lane_, d, r).start()
                d_copy(lane_, d, r, 0).start()
        if r > 1:
            finish(r - 1)
        if r in work:
            work[r]()
        if r == first_vit:
            images()
            ready(0)
            for i in range(1, r - 1):
                ready(i)
            vit_range(0, r - 1)
        elif r > first_vit:
            ready(r - 2)
            vit_range(r - 2, r - 1)
    finish(hops)
    ready(hops - 1)
    vit_range(hops - 1, hops)
    ready(hops)
    vit_range(hops, hops + 1)

    rows = arrived.shape[1]
    for k in range(RECV_MAX):
        at = lax.broadcasted_iota(jnp.int32, (rows, acc.shape[1]), 0)
        block = acc[k * rows : (k + 1) * rows, :]
        emb[k] = jnp.where(at < kept[k], block, 0.0).astype(BF16)

    drain(w.at[:, pl.ds(0, hops), pl.ds(0, 2), pl.ds(0, xrows)], x_send)
    drain(w.at[:, pl.ds(0, hops), pl.ds(0, 2), pl.ds(0, xrows)], d_send)
    drain(w.at[:, pl.ds(0, 1), pl.ds(0, 2)], da_send)
    if paired:
        drain(w.at[:, pl.ds(0, hops), pl.ds(0, 2), pl.ds(0, zrows)], z_send)
        drain(w.at[:, pl.ds(0, hops), pl.ds(0, 2), pl.ds(0, zrows)], dz_send)
    drain(outgoing.at[pl.ds(0, n_dp - 1)], a_sem.at[0])
    drain(meta_in.at[pl.ds(0, n_dp - 1)], m_sem.at[0])
    drain(rs_src.at[pl.ds(0, n_tp - 1)], rs_sem.at[0])
    drain(ag_dst.at[pl.ds(0, n_tp - 1)], ag_sem.at[0])


def local(sizes, *args):
    (
        patches,
        patch_counts,
        encoder_index,
        vit_gain,
        vit_up,
        vit_down,
        queries,
        cache_keys,
        cache_values,
        new_keys,
        new_values,
        kv_lengths,
        out_weight,
    ) = args
    n_tp, n_dp, paired = sizes
    slots, rows, width = patches.shape
    units = vit_down.shape[0]
    half = units // 2
    ring = n_tp // CORES
    seqs = queries.shape[0]
    columns = out_weight.shape[1]
    smem = pl.BlockSpec(memory_space=pltpu.SMEM)
    vmem = pl.BlockSpec(memory_space=pltpu.VMEM)
    hbm = pl.BlockSpec(memory_space=pl.ANY)
    dma = pltpu.SemaphoreType.DMA
    return pl.pallas_call(
        functools.partial(kernel, sizes),
        out_shape=(
            jax.ShapeDtypeStruct((RECV_MAX, rows, width), BF16),
            jax.ShapeDtypeStruct((seqs, columns), BF16),
        ),
        in_specs=[smem, smem, smem, hbm, vmem, hbm, hbm, vmem, hbm, hbm, vmem, vmem, hbm],
        out_specs=(vmem, vmem),
        scratch_shapes=[
            pltpu.VMEM((2, ring, 4, half, width), BF16),
            pltpu.VMEM(vit_up.shape, BF16),
            pltpu.VMEM(patches.shape, BF16),
            pltpu.VMEM((n_dp, rows, width), BF16),
            pltpu.VMEM((n_dp, rows, width), BF16),
            pltpu.VMEM(cache_keys.shape, BF16),
            pltpu.VMEM(cache_values.shape, BF16),
            pltpu.VMEM(out_weight.shape, BF16),
            pltpu.VMEM((8, 128), jnp.int32),
            pltpu.VMEM((n_dp, 8, 128), jnp.int32),
            pltpu.SMEM((n_dp, 8, 128), jnp.int32),
            pltpu.VMEM((n_tp, 16, 128), F32),
            pltpu.VMEM((n_tp, 16, 128), F32),
            pltpu.VMEM((n_tp, 8, 128), F32),
            pltpu.VMEM((n_tp, 8, 128), F32),
            pltpu.VMEM((n_tp, 8, 128), F32),
            pltpu.VMEM((RECV_MAX * rows, width), BF16),
            pltpu.VMEM((RECV_MAX * rows, width), F32),
            dma((8,)),
            dma((2, 2, ring - 1)),
            dma((2, 2, ring)),
            dma((2, 2, ring, 2)),
            dma,
            dma,
            dma,
            dma,
            dma,
            dma((2,)),
            dma((2,)),
            dma((2,)),
            dma((2,)),
        ],
        compiler_params=pltpu.CompilerParams(
            collective_id=0, has_side_effects=True, vmem_limit_bytes=62 * 1024 * 1024
        ),
        name="step",
    )(
        patch_counts,
        encoder_index,
        kv_lengths,
        patches,
        vit_gain.reshape(1, width),
        vit_up,
        vit_down,
        queries,
        cache_keys,
        cache_values,
        new_keys,
        new_values,
        out_weight,
    )


def solution(mesh):
    groups = mesh.shape["group"]
    sizes = (mesh.shape["tp"], mesh.shape["dp"], groups % 2 == 0)
    return jax.shard_map(
        functools.partial(local, sizes),
        mesh=mesh,
        in_specs=(
            P(("group", "tp", "dp"), None, None),
            P(("group", "tp", "dp")),
            P(("group", "tp", "dp")),
            P(),
            P(None, "tp"),
            P("tp", None),
            P(("group", "dp"), None, None),
            P(("group", "dp"), None, "tp", None),
            P(("group", "dp"), None, "tp", None),
            P(("group", "dp"), None, None),
            P(("group", "dp"), None, None),
            P(("group", "dp")),
            P(None, "tp"),
        ),
        out_specs=(P(("group", "tp", "dp"), None, None), P(("group", "dp"), "tp")),
        check_vma=False,
    )
```

time: 203 us -> 140 us (0.69)
  Pallas kernels: 0 us -> 132 us
  waiting for transfers between devices: 62 us -> 0 us
  blocking collectives: 36.8 us -> 0 us
  starting transfers between devices: 32.8 us -> 0 us
  matrix products: 32.2 us -> 0 us
  between operations: 14.3 us -> 0.64 us
  other arithmetic: 9.94 us -> 0 us
  local copies, waits for them, and re-layouts: 14.3 us -> 6.98 us
    pallas_call x0 -> x1, Pallas kernels: none -> 132 us  [local(): pl.pallas_call(functools.partial(kernel, sizes), out_shape=(jax.ShapeDtyp...]
    all_gather x1 -> x0, waiting for transfers between devices: 39.2 us -> none  [gather_turned(): whole = lax.all_gather(both, axis, axis=0, tiled=True)]
    all_gather x2 -> x0, blocking collectives: 36.8 us -> none  [over_pieces(): blocks = lax.all_gather(array, axis).astype(jnp.float32)]
    all_to_all x3 -> x0, starting transfers between devices: 32.7 us -> none  [the longest x1 14.4 us: from_everyone(): return lax.all_to_all(copies, axis, split_axis=0, concat_axis=0, tiled=True)]
    dot_general x7 -> x0, matrix products: 32.2 us -> none  [the longest x1 20.8 us: vit_block(): branch = jnp.dot(hidden, down_whole, preferred_element_type=jnp.float32)]
    all_to_all x3 -> x0, waiting for transfers between devices: 22.8 us -> none  [the longest x1 17.7 us: place_images(): lax.all_to_all(outgoing, 'dp', split_axis=0, concat_axis=0, tiled=True)]
    convert_element_type x2 -> x0, local copies, waits for them, and re-layouts: 5.26 us -> none  [the longest x1 4.57 us: vit_block(): xfloat = block_rows.astype(jnp.float32)]
    reduce_sum x7 -> x0, other arithmetic: 4.19 us -> none  [the longest x1 1.92 us: vit_block(): spread = jnp.mean(center * center, axis=-1, keepdims=True)]
  transfers between devices with their start and end apart: 4 -> 0, of which waited for: 4 -> 0; matrix products, arithmetic and copies ran while one was open for 16% -> 0% of each run, Pallas kernels for 0% -> 0%
where the time goes in v1:
time: 140 us
  Pallas kernels  132 us (94%)
  local copies, waits for them, and re-layouts  6.98 us (5%)
    pallas_call x1, Pallas kernels, local(): pl.pallas_call(functools.partial(kernel, sizes), out_shape=(jax.ShapeDtyp...  132 us
    unnamed x3, local copies, waits for them, and re-layouts  5.69 us

profile of v1, /device:TPU:513, one launch (start us, length us, event | category | flops | bytes accessed | tf_op | source)
XLA Modules:
  0.0 139.6 jit_solution(3631085830757826265)
XLA Ops:
  0.6 1.3 reshape.7.gain
  1.9 2.2 %copy.15.up = bf16[1280,320]{1,0:T(8,128)(2,1)} copy(bf16[1280,320]{0,1:T(8,128)(2,1)} %param.17) | data formatting | bytes 1638400 | tf_op args[4]
  4.1 132.0 %step.1 = (bf16[3,128,1280]{2,1,0:T(8,128)(2,1)}, bf16[4,512]{1,0:T(4,128)(2,1)}) custom-call(s32[4]{0:T(128)} %counts.1, s32[4]{0:T(128)} %enc.1, s32[4]{0:T(128)} %lens.1, bf16[4,128,1280]{2,1,0:T(8,128)(2,1)} %patches.1, f32[1,1280]{1,0:T(1,128)} %reshape.7.gain, bf16[1280,320]{1,0:T(8,128)(2,1)} %copy.15.up, bf16[320,1280]{1,0:T(8,128)(2,1)} %down.1, ...), custom_call_target="tpu_custom_call" | custom-call | tf_op jit(solution)/shard_map/step/pallas_call | solution.py:429
  136.1 2.2 %copy.18 = bf16[3,128,1280]{2,1,0:T(8,128)(2,1)} copy(bf16[3,128,1280]{2,1,0:T(8,128)(2,1)} %get-tuple-element.4) | data formatting | bytes 1966080
  138.4 1.3 copy.19

commit v2 on v1

v2 whole, which is shorter than its diff:
```python
import functools

import jax
import jax.numpy as jnp
from jax import lax
from jax.experimental import pallas as pl
from jax.experimental.pallas import tpu as pltpu
from jax.sharding import PartitionSpec as P

MESH = pl.DeviceIdType.MESH
RECV_MAX = 3
CORES = 2
PARTS = 2
F32 = jnp.float32
BF16 = jnp.bfloat16


def rcopy(src, dst, send, recv, **where):
    return pltpu.make_async_remote_copy(
        src_ref=src,
        dst_ref=dst,
        send_sem=send,
        recv_sem=recv,
        device_id=where,
        device_id_type=MESH,
    )


def drain(ref, sem):
    pltpu.make_async_copy(ref, ref, sem).wait()


def split_rows(half):
    tiles = half // 16
    zrows, yrows = tiles * 3 // 10 * 16, tiles // 10 * 16
    return zrows, yrows, half - 2 * zrows - 2 * yrows


def kernel(
    sizes,
    counts,
    enc,
    lens,
    patches,
    gain,
    up,
    down,
    q,
    keys,
    values,
    nk,
    nv,
    ow,
    emb,
    dec,
    w,
    pv,
    outgoing,
    arrived_a,
    arrived_b,
    kv,
    vv,
    owv,
    meta_out,
    meta_in,
    meta_s,
    rs_src,
    rs_dst,
    ag_dst,
    own_buf,
    nv_buf,
    normed,
    turned,
    acc,
    part_out,
    part_in,
    local_sem,
    x_recv,
    z_recv,
    y_recv,
    x_send,
    z_send,
    y_send,
    a_send,
    a_recv,
    m_sem,
    rs_sem,
    ag_sem,
    tok_send,
    tok_recv,
    part_send,
    part_recv,
):
    n_tp, n_dp = sizes
    ring = n_tp // CORES
    hops = ring - 1
    half = w.shape[3]
    zrows, yrows, drows = split_rows(half)
    t = lax.axis_index("tp")
    y = lax.axis_index("dp")
    g = lax.axis_index("group")
    gpar = lax.rem(g, 2)
    ypar = lax.rem(y, 2)
    core = lax.rem(t, CORES)
    right = lax.rem(t + CORES, n_tp)
    left = lax.rem(t + n_tp - CORES, n_tp)
    sib = t + 1 - 2 * core
    peer = g + 1 - 2 * gpar
    above, below = lax.rem(y + 1, n_dp), lax.rem(y + n_dp - 1, n_dp)
    zmine = pl.multiple_of(gpar * (half - zrows), 16)
    zother = pl.multiple_of((1 - gpar) * (half - zrows), 16)
    ymine = pl.multiple_of(zrows + ypar * (yrows + drows), 16)
    yother = pl.multiple_of(zrows + (1 - ypar) * (yrows + drows), 16)
    lanes = ((zmine, zrows), (ymine, yrows), (zrows + yrows, drows))
    slots, rows, width = patches.shape
    few = rows // PARTS
    arrived = (arrived_a, arrived_b)

    barrier = pltpu.get_barrier_semaphore()
    for d in range(1, n_tp):
        pl.semaphore_signal(
            barrier, inc=1, device_id={"tp": lax.rem(t + d, n_tp)}, device_id_type=MESH
        )
    for d in range(1, n_dp):
        pl.semaphore_signal(
            barrier, inc=1, device_id={"dp": lax.rem(y + d, n_dp)}, device_id_type=MESH
        )
    pl.semaphore_signal(barrier, inc=1, device_id={"group": peer}, device_id_type=MESH)

    loads = [
        pltpu.make_async_copy(up.at[pl.ds(0, half)], w.at[0, 0, 0], local_sem.at[0]),
        pltpu.make_async_copy(up.at[pl.ds(half, half)], w.at[0, 0, 1], local_sem.at[8]),
        pltpu.make_async_copy(down.at[pl.ds(0, half)], w.at[1, 0, 0], local_sem.at[1]),
        pltpu.make_async_copy(down.at[pl.ds(half, half)], w.at[1, 0, 1], local_sem.at[2]),
        pltpu.make_async_copy(patches, pv, local_sem.at[3]),
        pltpu.make_async_copy(keys, kv, local_sem.at[4]),
        pltpu.make_async_copy(values, vv, local_sem.at[5]),
        pltpu.make_async_copy(ow, owv, local_sem.at[6]),
    ]
    for load in loads:
        load.start()

    row = lax.broadcasted_iota(jnp.int32, (8, 128), 0)
    lane = lax.broadcasted_iota(jnp.int32, (8, 128), 1)
    meta = jnp.zeros((8, 128), jnp.int32)
    for s in range(slots):
        meta = jnp.where((row == 0) & (lane == s), counts[s], meta)
        meta = jnp.where((row == 1) & (lane == s), enc[s], meta)
    meta_out[...] = meta
    meta_in[y] = meta

    pl.semaphore_wait(barrier, n_tp + n_dp - 1)

    def x_copy(k, d, r):
        rows = pl.ds(*lanes[k])
        return rcopy(
            w.at[:, r, d, rows],
            w.at[:, r + 1, d, rows],
            x_send,
            x_recv.at[k, d, r],
            tp=right if d == 0 else left,
        )

    def z_copy(d, r):
        at = w.at[:, r, d, pl.ds(zmine, zrows)]
        return rcopy(at, at, z_send, z_recv.at[d, r], group=peer)

    def y_copy(d, r):
        at = w.at[:, r, d, pl.ds(ymine, yrows)]
        return rcopy(at, at, y_send, y_recv.at[d, r], dp=above if d == 0 else below)

    for load in loads[:4]:
        load.wait()
    for k in (0, 1):
        for d in (0, 1):
            x_copy(k, d, 0).start()

    loads[4].wait()

    def stage(e, carry):
        slot = jnp.int32(0)
        for s in range(slots):
            slot = slot + jnp.where((counts[s] > 0) & (enc[s] == e), s, 0)
        outgoing[e] = pv[slot]
        return carry

    lax.fori_loop(0, n_dp, stage, 0)
    for d in range(1, n_dp):
        to = lax.rem(y + d, n_dp)
        rcopy(meta_out, meta_in.at[y], m_sem.at[0], m_sem.at[1], dp=to).start()
    far_first = sorted(range(1, n_dp), key=lambda d: -min(d, n_dp - d))
    for p in range(PARTS):
        for d in far_first:
            to = lax.rem(y + d, n_dp)
            rcopy(
                outgoing.at[to, pl.ds(p * few, few)],
                arrived[p].at[y],
                a_send,
                a_recv.at[p],
                dp=to,
            ).start()
    for p in range(PARTS):
        arrived[p][y] = outgoing[y, p * few : (p + 1) * few, :]

    seqs, kvh, span, hd = kv.shape
    per = q.shape[1] // kvh
    scale = hd**-0.5
    own_heads = (kvh * per) // n_tp

    def attend_local():
        loads[5].wait()
        loads[6].wait()
        wide = lax.broadcasted_iota(jnp.int32, (per, 128), 1)
        for s in range(seqs):
            pos = t * span + lax.broadcasted_iota(jnp.int32, (per, span), 1)
            valid = pos < lens[s]
            for h in range(kvh):
                query = q[s, h * per : (h + 1) * per, :]
                scores = (
                    lax.dot_general(
                        query, kv[s, h], (((1,), (1,)), ((), ())), preferred_element_type=F32
                    )
                    * scale
                )
                scores = jnp.where(valid, scores, -1e30)
                own = (
                    jnp.sum(
                        query.astype(F32) * nk[s, h : h + 1, :].astype(F32), axis=1, keepdims=True
                    )
                    * scale
                )
                top = jnp.maximum(jnp.max(scores, axis=1, keepdims=True), own)
                weights = jnp.exp(scores - top)
                total = jnp.sum(weights, axis=1, keepdims=True)
                mix = jnp.dot(weights.astype(BF16), vv[s, h], preferred_element_type=F32)
                stats = jnp.where(wide < 64, top, total)
                ownw = jnp.broadcast_to(own, (per, 128))
                fresh = nv[s, h : h + 1, :].astype(F32)
                for i in range(per):
                    head = h * per + i
                    p, j = head // own_heads, head % own_heads
                    at = seqs * j + s
                    rs_src[p, at : at + 1, :] = mix[i : i + 1, :]
                    rs_src[p, 8 + at : 9 + at, :] = stats[i : i + 1, :]
                    own_buf[p, at : at + 1, :] = ownw[i : i + 1, :]
                    nv_buf[p, at : at + 1, :] = fresh
        rs_dst[t] = rs_src[t]
        for d in range(1, n_tp):
            to = lax.rem(t + d, n_tp)
            rcopy(rs_src.at[to], rs_dst.at[t], rs_sem.at[0], rs_sem.at[1], tp=to).start()

    def attend_merge():
        some = pl.ds(0, n_tp - 1)
        drain(rs_dst.at[some], rs_sem.at[1])
        own = own_buf[t][:, 0:1]
        tops = [rs_dst[p, 8:16, 0:1] for p in range(n_tp)]
        top = own
        for m in tops:
            top = jnp.maximum(top, m)
        own_weight = jnp.exp(own - top)
        total = own_weight
        mixed = own_weight.astype(BF16).astype(F32) * nv_buf[t]
        for p in range(n_tp):
            factor = jnp.exp(tops[p] - top)
            total = total + rs_dst[p, 8:16, 64:65] * factor
            mixed = mixed + rs_dst[p, 0:8, :] * factor
        ag_dst[t] = (mixed / total).astype(BF16).astype(F32)
        for d in range(1, n_tp):
            to = lax.rem(t + d, n_tp)
            rcopy(ag_dst.at[t], ag_dst.at[t], ag_sem.at[0], ag_sem.at[1], tp=to).start()

    def project():
        loads[7].wait()
        drain(ag_dst.at[pl.ds(0, n_tp - 1)], ag_sem.at[1])
        wide = own_heads * hd
        total = jnp.zeros((8, owv.shape[1]), F32)
        which = lax.broadcasted_iota(jnp.int32, (8, hd), 0) // seqs
        for p in range(n_tp):
            block = ag_dst[p]
            lhs = jnp.concatenate(
                [jnp.where(which == j, block, 0.0) for j in range(own_heads)], axis=1
            ).astype(BF16)
            total = total + jnp.dot(
                lhs, owv[p * wide : (p + 1) * wide, :], preferred_element_type=F32
            )
        out = total[0:seqs]
        for j in range(1, own_heads):
            out = out + total[j * seqs : (j + 1) * seqs]
        dec[...] = out.astype(BF16)

    picked, kept = [], []
    both = CORES * RECV_MAX * few
    mine = RECV_MAX * few

    def plan():
        drain(meta_in.at[pl.ds(0, n_dp - 1)], m_sem.at[1])
        small = pltpu.make_async_copy(meta_in, meta_s, local_sem.at[7])
        small.start()
        small.wait()
        found = jnp.int32(0)
        pick = [jnp.int32(0)] * RECV_MAX
        keep = [jnp.int32(0)] * RECV_MAX
        for src in range(n_dp):
            count = jnp.int32(0)
            for s in range(slots):
                c = meta_s[src, 0, s]
                count = count + jnp.where((c > 0) & (meta_s[src, 1, s] == y), c, 0)
            for k in range(RECV_MAX):
                hit = (count > 0) & (found == k)
                pick[k] = jnp.where(hit, src, pick[k])
                keep[k] = jnp.where(hit, count, keep[k])
            found = found + jnp.where(count > 0, 1, 0)
        picked.extend(pick)
        kept.extend(keep)

    def tokens(p):
        here, there = pl.ds(0, mine), pl.ds(mine, mine)
        return rcopy(
            normed.at[p, here], normed.at[p, there], tok_send, tok_recv.at[p], tp=sib
        )

    def images(p):
        drain(arrived[p].at[pl.ds(0, n_dp - 1)], a_recv.at[p])
        for k in range(RECV_MAX):
            at = slice(k * few, (k + 1) * few)
            x = arrived[p][picked[k]].astype(F32)
            acc[p, at, :] = x
            center = x - jnp.mean(x, axis=1, keepdims=True)
            spread = jnp.mean(center * center, axis=1, keepdims=True)
            n = center * lax.rsqrt(spread + 1e-06) * gain[...].reshape(1, width)
            normed[p, at, :] = n.astype(BF16)
        tokens(p).start()
        acc[p, mine:both, :] = jnp.zeros((both - mine, width), F32)

    def turn(p):
        drain(normed.at[p, pl.ds(0, mine)], tok_recv.at[p])
        turned[p] = jnp.transpose(normed[p].astype(F32)).astype(BF16)

    def vit(r, count, p):
        units = count * w.shape[2] * half
        a = w[0, pl.ds(r, count)].reshape(units, width)
        b = w[1, pl.ds(r, count)].reshape(units, width)
        pre = jnp.dot(a, turned[p], preferred_element_type=F32)
        hidden = jnp.transpose(pre * jax.nn.sigmoid(1.702 * pre)).astype(BF16)
        acc[p] += jnp.dot(hidden, b, preferred_element_type=F32)

    def vit_range(lo, hi, p):
        count = 2 if (hi - lo) % 2 == 0 else 1

        def body(i, carry):
            vit(lo + i * count, count, p)
            return carry

        lax.fori_loop(0, (hi - lo) // count, body, 0)

    seen = set()

    def ready(r):
        if r == 0 or r in seen:
            return
        seen.add(r)
        for d in (0, 1):
            drain(w.at[:, r, d, pl.ds(zother, zrows)], z_recv.at[d, r])
            drain(w.at[:, r, d, pl.ds(yother, yrows)], y_recv.at[d, r])

    def compute(lo, hi, p):
        for r in range(lo, hi):
            ready(r)
        vit_range(lo, hi, p)

    def part(p):
        return rcopy(part_out.at[p], part_in.at[p], part_send, part_recv.at[p], tp=sib)

    def arrive(k, d, r):
        drain(w.at[:, r, d, pl.ds(*lanes[k])], x_recv.at[k, d, r - 1])
        if r < hops:
            x_copy(k, d, r).start()

    last = hops
    work = {
        1: [attend_local],
        2: [attend_merge],
        3: [project, plan],
        last - 3: [lambda: images(0)],
        last - 2: [lambda: turn(0), lambda: compute(0, last - 3, 0)],
        last - 1: [
            lambda: images(1),
            lambda: compute(last - 3, last - 1, 0),
            lambda: turn(1),
        ],
        last: [lambda: compute(0, last - 3, 1), lambda: compute(last - 3, last - 1, 1)],
    }
    for r in range(1, hops + 1):
        for d in (0, 1):
            arrive(0, d, r)
            z_copy(d, r).start()
        for d in (0, 1):
            arrive(1, d, r)
            y_copy(d, r).start()
        for d in (0, 1):
            if r == 1:
                x_copy(2, d, 0).start()
            else:
                arrive(2, d, r - 1)
        for task in work.get(r, ()):
            task()
    for p in range(PARTS):
        compute(last - 1, last, p)
    for d in (0, 1):
        arrive(2, d, hops)
    for p in range(PARTS):
        compute(last, last + 1, p)
        part_out[p] = acc[p, mine:both, :].astype(BF16)
        part(p).start()
    for p in range(PARTS):
        drain(part_in.at[p], part_recv.at[p])
        which = p * few + lax.broadcasted_iota(jnp.int32, (few, width), 0)
        for k in range(RECV_MAX):
            at = slice(k * few, (k + 1) * few)
            block = acc[p, at, :] + part_in[p, at, :].astype(F32)
            emb[k, p * few : (p + 1) * few, :] = jnp.where(which < kept[k], block, 0.0).astype(BF16)

    sent = zrows + yrows + drows
    drain(w.at[:, pl.ds(0, hops), :, pl.ds(0, sent)], x_send)
    drain(w.at[:, pl.ds(0, hops), :, pl.ds(0, zrows)], z_send)
    drain(w.at[:, pl.ds(0, hops), :, pl.ds(0, yrows)], y_send)
    drain(outgoing.at[pl.ds(0, n_dp - 1)], a_send)
    drain(meta_in.at[pl.ds(0, n_dp - 1)], m_sem.at[0])
    drain(rs_src.at[pl.ds(0, n_tp - 1)], rs_sem.at[0])
    drain(ag_dst.at[pl.ds(0, n_tp - 1)], ag_sem.at[0])
    drain(normed.at[:, pl.ds(0, mine)], tok_send)
    drain(part_out, part_send)


def local(sizes, *args):
    (
        patches,
        patch_counts,
        encoder_index,
        vit_gain,
        vit_up,
        vit_down,
        queries,
        cache_keys,
        cache_values,
        new_keys,
        new_values,
        kv_lengths,
        out_weight,
    ) = args
    n_tp, n_dp = sizes
    slots, rows, width = patches.shape
    units = vit_down.shape[0]
    half = units // 2
    ring = n_tp // CORES
    mine = RECV_MAX * rows // PARTS
    seqs = queries.shape[0]
    columns = out_weight.shape[1]
    smem = pl.BlockSpec(memory_space=pltpu.SMEM)
    vmem = pl.BlockSpec(memory_space=pltpu.VMEM)
    hbm = pl.BlockSpec(memory_space=pl.ANY)
    dma = pltpu.SemaphoreType.DMA
    return pl.pallas_call(
        functools.partial(kernel, sizes),
        out_shape=(
            jax.ShapeDtypeStruct((RECV_MAX, rows, width), BF16),
            jax.ShapeDtypeStruct((seqs, columns), BF16),
        ),
        in_specs=[smem, smem, smem, hbm, vmem, hbm, hbm, vmem, hbm, hbm, vmem, vmem, hbm],
        out_specs=(vmem, vmem),
        scratch_shapes=[
            pltpu.VMEM((2, ring, 2, half, width), BF16),
            pltpu.VMEM(patches.shape, BF16),
            pltpu.VMEM((n_dp, rows, width), BF16),
            pltpu.VMEM((n_dp, rows // PARTS, width), BF16),
            pltpu.VMEM((n_dp, rows // PARTS, width), BF16),
            pltpu.VMEM(cache_keys.shape, BF16),
            pltpu.VMEM(cache_values.shape, BF16),
            pltpu.VMEM(out_weight.shape, BF16),
            pltpu.VMEM((8, 128), jnp.int32),
            pltpu.VMEM((n_dp, 8, 128), jnp.int32),
            pltpu.SMEM((n_dp, 8, 128), jnp.int32),
            pltpu.VMEM((n_tp, 16, 128), F32),
            pltpu.VMEM((n_tp, 16, 128), F32),
            pltpu.VMEM((n_tp, 8, 128), F32),
            pltpu.VMEM((n_tp, 8, 128), F32),
            pltpu.VMEM((n_tp, 8, 128), F32),
            pltpu.VMEM((PARTS, CORES * mine, width), BF16),
            pltpu.VMEM((PARTS, width, CORES * mine), BF16),
            pltpu.VMEM((PARTS, CORES * mine, width), F32),
            pltpu.VMEM((PARTS, mine, width), BF16),
            pltpu.VMEM((PARTS, mine, width), BF16),
            dma((9,)),
            dma((3, 2, ring - 1)),
            dma((2, ring)),
            dma((2, ring)),
            dma,
            dma,
            dma,
            dma,
            dma((PARTS,)),
            dma((2,)),
            dma((2,)),
            dma((2,)),
            dma,
            dma((PARTS,)),
            dma,
            dma((PARTS,)),
        ],
        compiler_params=pltpu.CompilerParams(
            collective_id=0, has_side_effects=True, vmem_limit_bytes=62 * 1024 * 1024
        ),
        name="step",
    )(
        patch_counts,
        encoder_index,
        kv_lengths,
        patches,
        vit_gain,
        vit_up.T,
        vit_down,
        queries,
        cache_keys,
        cache_values,
        new_keys,
        new_values,
        out_weight,
    )


def solution(mesh):
    assert mesh.shape["group"] % 2 == 0 and mesh.shape["dp"] % 2 == 0
    sizes = (mesh.shape["tp"], mesh.shape["dp"])
    return jax.shard_map(
        functools.partial(local, sizes),
        mesh=mesh,
        in_specs=(
            P(("group", "tp", "dp"), None, None),
            P(("group", "tp", "dp")),
            P(("group", "tp", "dp")),
            P(),
            P(None, "tp"),
            P("tp", None),
            P(("group", "dp"), None, None),
            P(("group", "dp"), None, "tp", None),
            P(("group", "dp"), None, "tp", None),
            P(("group", "dp"), None, None),
            P(("group", "dp"), None, None),
            P(("group", "dp")),
            P(None, "tp"),
        ),
        out_specs=(P(("group", "tp", "dp"), None, None), P(("group", "dp"), "tp")),
        check_vma=False,
    )
```

time: 140 us -> 132 us (0.943)
  Pallas kernels: 132 us -> 127 us
  local copies, waits for them, and re-layouts: 6.98 us -> 3.48 us
    pallas_call x1, Pallas kernels: 132 us -> 127 us  [local(): pl.pallas_call(functools.partial(kernel, sizes), out_shape=(jax.ShapeDtyp...]
    unnamed x3 -> x2, local copies, waits for them, and re-layouts: 5.69 us -> 3.48 us
where the time goes in v2:
time: 132 us
  Pallas kernels  127 us (96%)
  local copies, waits for them, and re-layouts  3.48 us (3%)
    pallas_call x1, Pallas kernels, local(): pl.pallas_call(functools.partial(kernel, sizes), out_shape=(jax.ShapeDtyp...  127 us
    unnamed x2, local copies, waits for them, and re-layouts  3.48 us

profile of v2, /device:TPU:513, one launch (start us, length us, event | category | flops | bytes accessed | tf_op | source)
XLA Modules:
  0.0 131.6 jit_solution(2293936258429552337)
XLA Ops:
  0.6 127.4 %step.1 = (bf16[3,128,1280]{2,1,0:T(8,128)(2,1)}, bf16[4,512]{1,0:T(4,128)(2,1)}) custom-call(s32[4]{0:T(128)} %counts.1, s32[4]{0:T(128)} %enc.1, s32[4]{0:T(128)} %lens.1, bf16[4,128,1280]{2,1,0:T(8,128)(2,1)} %patches.1, f32[1280]{0:T(1024)} %gain.1, bf16[320,1280]{1,0:T(8,128)(2,1)} %bitcast.1, bf16[320,1280]{1,0:T(8,128)(2,1)} %down.1, ...), custom_call_target="tpu_custom_call" | custom-call | tf_op jit(solution)/shard_map/step/pallas_call | solution.py:463
  128.1 2.2 %copy.17 = bf16[3,128,1280]{2,1,0:T(8,128)(2,1)} copy(bf16[3,128,1280]{2,1,0:T(8,128)(2,1)} %get-tuple-element.4) | data formatting | bytes 1966080
  130.3 1.3 copy.18
